TPU v7x, 32 devices: a whole 2x2x4 slice. The times are simulated.
32 devices in a mesh: section: 2 (over core), dev: 16 (over z, y, x).
Axes of the slice: x: 2, y: 2, z: 4, core: 2. Of those that a mesh axis runs over, the one named last changes fastest.
Arguments:
- indices: int32 [2048, 32, 8], P(('section', 'dev')), may hold values from 0 to 32767
- pool_len: int32 [32], replicated, may hold values from 1 to 8
- tables: bfloat16 [1048576, 128], P(('section', 'dev')), may hold values from -3 to 3
- w_first: bfloat16 [4096, 4096], P('dev', 'section'), may hold values from -0.09375 to 0.09375
- b_first: bfloat16 [4096], P('section'), may hold values from -3 to 3
- w_out: bfloat16 [4096], P('section'), may hold values from -0.09375 to 0.09375
Outputs:
- logits: float32 [2048], P('dev')
Inputs may be any that keep to these rules, and one draw needn't show every extreme that they name: `indices`: ids of rows of the table named by the second index.
All inputs are finite; a program needn't handle non-finite values.
Results may differ from a plain program's by a relative error of at most 0.0095.
Values may be sent and summed in bfloat16 or wider, within the bound.
A program may use at most 128 MiB of HBM per device.

v0:
```python
import jax
import jax.numpy as jnp
from jax import lax
from jax.sharding import PartitionSpec as P


def body(indices, pool_len, tables, w_first, b_first, w_out):
    sec_count = lax.axis_size("section")
    dev_count = lax.axis_size("dev")
    devices = sec_count * dev_count
    dev_rows, n_tables, pool_size = indices.shape
    rows_dev, emb_width = tables.shape
    row_split = devices // n_tables
    position = lax.axis_index("section") * dev_count + lax.axis_index("dev")
    table_id = position // row_split
    first_row = position % row_split * rows_dev
    outgoing = jnp.repeat(indices, row_split, axis=1)
    arrived = lax.all_to_all(outgoing, ("section", "dev"), split_axis=1, concat_axis=0, tiled=True)
    all_rows = devices * dev_rows
    wanted = arrived.reshape(all_rows, pool_size) - first_row
    live_slots = jnp.sum(jnp.where(jnp.arange(n_tables) == table_id, pool_len, 0))
    usable = (wanted >= 0) & (wanted < rows_dev) & (jnp.arange(pool_size)[None, :] < live_slots)
    safe_rows = jnp.where(usable, wanted, 0)
    looked = jnp.take(tables, safe_rows, axis=0)
    picked = jnp.where(usable[:, :, None], looked, jnp.zeros((), jnp.bfloat16))
    partial_value = jnp.sum(picked.astype(jnp.float32), axis=1).astype(jnp.bfloat16)
    ordered = jnp.transpose(
        partial_value.reshape(dev_count, sec_count, dev_rows, emb_width), (1, 0, 2, 3)
    )
    received = lax.all_to_all(
        ordered.reshape(devices, dev_rows, emb_width),
        ("section", "dev"),
        split_axis=0,
        concat_axis=0,
        tiled=True,
    )
    summed = jnp.sum(
        received.reshape(n_tables, row_split, dev_rows, emb_width).astype(jnp.float32), axis=1
    )
    features = jnp.transpose(summed.astype(jnp.bfloat16), (1, 0, 2)).reshape(
        dev_rows, n_tables * emb_width
    )
    samples = lax.all_gather(features, "section", axis=0, tiled=True)
    whole_weights = lax.all_gather(w_first, "dev", axis=0, tiled=True)
    pre_act = jnp.dot(samples, whole_weights, preferred_element_type=jnp.float32)
    hidden = jnp.maximum(pre_act + b_first.astype(jnp.float32)[None, :], 0.0)
    logit_part = jnp.sum(hidden * w_out.astype(jnp.float32)[None, :], axis=1)
    return lax.psum(logit_part, "section")


def solution(mesh):
    placed = (
        P(("section", "dev"), None, None),
        P(),
        P(("section", "dev"), None),
        P("dev", "section"),
        P("section"),
        P("section"),
    )
    return jax.shard_map(body, mesh=mesh, in_specs=placed, out_specs=P("dev"), check_vma=False)
```

profile of v0, /device:TPU:19, one launch (start us, length us, event | category | flops | bytes accessed | tf_op | source)
XLA Modules:
  0.0 334.9 jit_solution(18316282832456618671)
XLA Ops:
  6.5 1.6 reshape.131
  8.2 6.2 %all-to-all-start = ((s32[32,1,512]{2,1,0:T(1,128)}), s32[32,1,512]{2,1,0:T(1,128)S(1)}, u32[]{:S(2)}, u32[]{:S(2)}) async-start(s32[32,1,512]{2,1,0:T(1,128)} %reshape.131), calls=%async_computation | async-start | bytes 131072 | tf_op jit(solution)/shard_map/all_to_all | solution.py:18
  14.4 1.3 fusion.5
  15.7 0.6 iota_compare_fusion
  16.4 2.2 all-to-all-done
  18.6 0.5 broadcast.97
  19.1 0.8 reduce.1
  19.9 0.1 reshape.132
  20.0 0.1 reshape.117
  20.1 0.1 reshape.118
  20.2 0.1 and_and_fusion
  20.3 0.4 copy.14
  20.8 0.4 copy.15
  21.3 0.3 copy.17
  21.7 0.5 reshape.124
  22.2 59.4 %gather_fusion = bf16[16384,128]{1,0:T(8,128)(2,1)} fusion(bf16[32768,128]{1,0:T(8,128)(2,1)} %param.8, s32[16384]{0:T(1024)S(1)} %broadcast_clamp_fusion), kind=kCustom, calls=%fused_computation | custom fusion | bytes 8454144 | tf_op jit(solution)/shard_map/jit(_take)/gather | solution.py:24
  81.6 12.6 %fusion.1 = bf16[2048,128]{1,0:T(8,128)(2,1)S(1)} fusion(bf16[16384,128]{1,0:T(8,128)(2,1)} %gather_fusion, pred[2048,8]{1,0:T(8,128)(4,1)S(1)} %copy.15, pred[2048,8]{1,0:T(8,128)(4,1)S(1)} %copy.14), kind=kLoop, calls=%fused_computation.3 | loop fusion | flops 6029312 | bytes 4751360 | tf_op jit(solution)/shard_map/reduce_sum | solution.py:26
  94.3 18.4 %all_to_all.20 = bf16[32,64,128]{2,1,0:T(8,128)(2,1)S(1)} all-to-all(bf16[32,64,128]{2,1,0:T(8,128)(2,1)S(1)} %bitcast.36), channel_id=1, replica_groups=mesh['section'=2,'dev'=16] {'section','dev'}, dimensions={0} | all-to-all | bytes 1048576 | tf_op jit(solution)/shard_map/all_to_all | solution.py:30
  112.6 0.9 copy_bitcast_fusion
  113.6 0.7 all-gather.5.cloned.1.call-update
  114.4 8.4 %all-gather.3.cloned.1.call-done = bf16[128,4096]{1,0:T(8,128)(2,1)} async-done(((bf16[64,4096]{1,0:T(8,128)(2,1)}), bf16[128,4096]{1,0:T(8,128)(2,1)}) %all-gather.3.cloned.1.call-update) | async-done | bytes 1048592 | tf_op jit(solution)/shard_map/all_gather | solution.py:43
  122.8 192.6 %all-gather.5.cloned.1.call-done = bf16[4096,2048]{1,0:T(8,128)(2,1)} async-done(((bf16[256,2048]{1,0:T(8,128)(2,1)}), bf16[4096,2048]{1,0:T(8,128)(2,1)}) %all-gather.5.cloned.1.call-update) | async-done | bytes 16777232 | tf_op jit(solution)/shard_map/all_gather | solution.py:44
  315.4 8.6 %fusion.4 = f32[128]{0:T(128)S(1)} fusion(bf16[128,4096]{1,0:T(8,128)(2,1)} %all-gather.3.cloned.1.call-done, bf16[4096,2048]{1,0:T(8,128)(2,1)} %all-gather.5.cloned.1.call-done, f32[2048]{0:T(1024)S(1)} %convert_element_type.12, f32[2048]{0:T(1024)S(1)} %convert_element_type.5), kind=kOutput, calls=%fused_computation.7 | convolution fusion | flops 2148532224 | bytes 17842688 | tf_op jit(solution)/shard_map/dot_general | solution.py:45
  324.0 4.0 %psum.7 = f32[128]{0:T(128)} all-reduce(f32[128]{0:T(128)S(1)} %fusion.4), channel_id=1, replica_groups=mesh['section'=2,'dev'=16] {'section'}, use_global_device_ids=true, to_apply=%region_3.4 | all-reduce | flops 128 | bytes 1024 | tf_op jit(solution)/shard_map/psum | solution.py:48
  (14 shorter events, 0.3 us)
Async XLA Ops:
  8.2 10.4 %all-to-all-start = ((s32[32,1,512]{2,1,0:T(1,128)}), s32[32,1,512]{2,1,0:T(1,128)S(1)}, u32[]{:S(2)}, u32[]{:S(2)}) async-start(s32[32,1,512]{2,1,0:T(1,128)} %reshape.131), calls=%async_computation | async-start | bytes 131072 | tf_op jit(solution)/shard_map/all_to_all | solution.py:18
  14.4 108.4 %all-gather.3.cloned.1.call-start = ((), (), s32[]{:S(2)}) async-start(), calls=%async_computation.2 | async-start | bytes 1572864 | tf_op jit(solution)/shard_map/all_gather | solution.py:43
  81.6 32.7 %copy-start = (bf16[2048]{0:T(1024)(128)(2,1)S(1)}, bf16[2048]{0:T(1024)(128)(2,1)}, u32[]{:S(2)}) copy-start(bf16[2048]{0:T(1024)(128)(2,1)} %param.11) | copy-start | bytes 12292
  81.6 32.7 %copy-start.1 = (bf16[2048]{0:T(1024)(128)(2,1)S(1)}, bf16[2048]{0:T(1024)(128)(2,1)}, u32[]{:S(2)}) copy-start(bf16[2048]{0:T(1024)(128)(2,1)} %param.10) | copy-start | bytes 12292
  113.6 201.8 %all-gather.5.cloned.1.call-start = ((), (), s32[]{:S(2)}) async-start(), calls=%async_computation.3 | async-start | bytes 17825792 | tf_op jit(solution)/shard_map/all_gather | solution.py:44
Sparse Core Ops, SparseCore 0:
  113.7 9.0 all-gather.2
  125.6 189.7 all-gather.4
where the time goes:
time: 337 us; the launch traced here: 335 us
  waiting for transfers between devices  204 us (61%)
  local copies, waits for them, and re-layouts  64.5 us (19%)
  blocking collectives  22.4 us (7%)
  other arithmetic  15.6 us (5%)
  between operations  13.5 us (4%)
  matrix products  8.58 us (3%)
  starting transfers between devices  6.27 us (2%)
    all_gather x1, waiting for transfers between devices, body(): whole_weights = lax.all_gather(w_first, 'dev', axis=0, tiled=True)  193 us
    gather x1, local copies, waits for them, and re-layouts, body(): looked = jnp.take(tables, safe_rows, axis=0)  59.4 us
    all_to_all x1, blocking collectives, body(): lax.all_to_all(ordered.reshape(devices, dev_rows, emb_width), ('section',...  18.4 us
    reduce_sum x1, other arithmetic, body(): jnp.sum(picked.astype(jnp.float32), axis=1).astype(jnp.bfloat16)  12.6 us
    dot_general x1, matrix products, body(): jnp.dot(samples, whole_weights, preferred_element_type=jnp.float32)  8.58 us
    all_gather x1, waiting for transfers between devices, body(): samples = lax.all_gather(features, 'section', axis=0, tiled=True)  8.45 us
  transfers between devices with their start and end apart: 3, of which 3 were waited for; matrix products, arithmetic and copies ran while one was open for 1% of the time, Pallas kernels for 0%

commit v1 on v0

--- a/solution.py
+++ b/solution.py
@@ -1,7 +1,209 @@
+import functools
+
 import jax
 import jax.numpy as jnp
 from jax import lax
+from jax.experimental import pallas as pl
+from jax.experimental.pallas import tpu as pltpu
 from jax.sharding import PartitionSpec as P
+
+VMEM_LIMIT = 60 * 1024 * 1024
+PLANE = 4
+
+
+def bag_kernel(table_chunks, bags_per_step, pool_size, table_ref, ids_ref, out_ref, staged, wide, sums, sems):
+    rows, _ = table_ref.shape
+    chunk = rows // table_chunks
+
+    def fetch(c):
+        return pltpu.make_async_copy(table_ref.at[pl.ds(c * chunk, chunk)], staged.at[c % 2], sems.at[c % 2])
+
+    fetch(0).start()
+    wide[pl.ds(rows, 8), :] = jnp.zeros((8, wide.shape[1]), jnp.float32)
+    for c in range(table_chunks):
+        if c + 1 < table_chunks:
+            fetch(c + 1).start()
+        fetch(c).wait()
+        step = 256
+
+        def widen(k, carry):
+            at = pl.multiple_of(k * step, step)
+            wide[pl.ds(c * chunk + at, step), :] = staged[c % 2, pl.ds(at, step), :].astype(jnp.float32)
+            return carry
+
+        lax.fori_loop(0, chunk // step, widen, 0)
+
+    def bags(r, carry):
+        for b in range(bags_per_step):
+            total = None
+            for p in range(pool_size):
+                row = wide[pl.ds(ids_ref[r, b * pool_size + p], 1), :]
+                total = row if total is None else total + row
+            sums[pl.ds(r * bags_per_step + b, 1), :] = total
+        return carry
+
+    lax.fori_loop(0, ids_ref.shape[0], bags, 0)
+    out_ref[...] = sums[...].astype(jnp.bfloat16)
+
+
+def pool_bags(table, ids, pool_size):
+    rows, emb = table.shape
+    bags_per_step = ids.shape[1] // pool_size
+    n_bags = ids.shape[0] * bags_per_step
+    chunks = 8
+    return pl.pallas_call(
+        functools.partial(bag_kernel, chunks, bags_per_step, pool_size),
+        out_shape=jax.ShapeDtypeStruct((n_bags, emb), jnp.bfloat16),
+        in_specs=[pl.BlockSpec(memory_space=pl.ANY), pl.BlockSpec(memory_space=pltpu.SMEM)],
+        out_specs=pl.BlockSpec(memory_space=pltpu.VMEM),
+        scratch_shapes=[
+            pltpu.VMEM((2, rows // chunks, emb), jnp.bfloat16),
+            pltpu.VMEM((rows + 8, emb), jnp.float32),
+            pltpu.VMEM((n_bags, emb), jnp.float32),
+            pltpu.SemaphoreType.DMA((2,)),
+        ],
+        compiler_params=pltpu.CompilerParams(vmem_limit_bytes=VMEM_LIMIT),
+        cost_estimate=pl.CostEstimate(flops=n_bags * pool_size * emb * 600, bytes_accessed=rows * emb * 2, transcendentals=0),
+        name="pool_bags",
+    )(table, ids)
+
+
+def dense_kernel(
+    secs, devs, pooled_ref, w_ref, b_ref, wo_ref, out_ref,
+    feats, pre, outgoing, incoming, mine, theirs,
+    fsend, frecv, psend, precv, lsend, lrecv,
+):
+    emb = pooled_ref.shape[1]
+    depth, hid = w_ref.shape
+    per_dev = depth // (devs // PLANE)
+    tables_dev = per_dev // emb
+    planes = devs // PLANE
+    group = pooled_ref.shape[0] // planes
+    block = group // PLANE
+    tiles = psend.shape[1]
+    tile = hid // tiles
+    sec, dev = lax.axis_index("section"), lax.axis_index("dev")
+    me = sec * devs + dev
+    plane, inner = dev // PLANE, dev % PLANE
+
+    barrier = pltpu.get_barrier_semaphore()
+    for k in range(1, secs * devs):
+        other = lax.rem(me + k, secs * devs)
+        pl.semaphore_signal(barrier, inc=1, device_id={"section": other // devs, "dev": lax.rem(other, devs)})
+    pl.semaphore_wait(barrier, secs * devs - 1)
+
+    owner = me // tables_dev
+    slot = owner // PLANE * tables_dev + lax.rem(me, tables_dev)
+    column = pl.ds(pl.multiple_of(slot * emb, emb), emb)
+    to_inner = lax.rem(owner, PLANE)
+    keeps = to_inner == inner
+    copies = []
+    for k in range(planes):
+        for c in range(secs):
+            to_plane = lax.rem(plane + k, planes)
+            to_sec = lax.rem(sec + c, secs)
+            src = pooled_ref.at[pl.ds(pl.multiple_of(to_plane * group, group), group), :]
+            dst = feats.at[:, column]
+            copy = pltpu.make_async_remote_copy(
+                src_ref=src, dst_ref=dst,
+                send_sem=fsend.at[k, c], recv_sem=frecv.at[slot],
+                device_id={"section": to_sec, "dev": to_plane * PLANE + to_inner},
+            )
+            if k == 0 and c == 0:
+                local = pltpu.make_async_copy(src, dst, frecv.at[slot])
+
+                @pl.when(keeps)
+                def _():
+                    local.start()
+
+                @pl.when(jnp.logical_not(keeps))
+                def _():
+                    copy.start()
+            else:
+                copy.start()
+            copies.append(copy)
+    for t in range(depth // emb):
+        part = feats.at[:, pl.ds(t * emb, emb)]
+        pltpu.make_async_copy(part, part, frecv.at[t]).wait()
+
+    partials = []
+    for n in range(tiles):
+        cols = pl.ds(n * tile, tile)
+        got = jnp.dot(feats[...], w_ref[:, cols], preferred_element_type=jnp.float32)
+        pre[:, cols] = got
+        outgoing[:, cols] = got.astype(jnp.bfloat16)
+        for k in range(1, PLANE):
+            to = lax.rem(inner + k, PLANE)
+            copy = pltpu.make_async_remote_copy(
+                src_ref=outgoing.at[pl.ds(pl.multiple_of(to * block, block), block), cols],
+                dst_ref=incoming.at[k - 1, :, cols],
+                send_sem=psend.at[k - 1, n], recv_sem=precv.at[k - 1, n],
+                device_id={"section": sec, "dev": plane * PLANE + to},
+            )
+            copy.start()
+            partials.append(copy)
+
+    acc = jnp.zeros((block, 128), jnp.float32)
+    own = pl.ds(pl.multiple_of(inner * block, block), block)
+    for n in range(tiles):
+        cols = pl.ds(n * tile, tile)
+        total = pre[own, cols]
+        for k in range(1, PLANE):
+            partials[n * (PLANE - 1) + k - 1].wait_recv()
+            total = total + incoming[k - 1, :, cols].astype(jnp.float32)
+        hidden = jnp.maximum(total + b_ref[:, cols].astype(jnp.float32), 0.0)
+        weighed = hidden * wo_ref[:, cols].astype(jnp.float32)
+        for q in range(tile // 128):
+            acc = acc + weighed[:, q * 128:(q + 1) * 128]
+    mine[...] = jnp.sum(acc.T, axis=0, keepdims=True)
+    swap = pltpu.make_async_remote_copy(
+        src_ref=mine, dst_ref=theirs, send_sem=lsend, recv_sem=lrecv,
+        device_id={"section": 1 - sec, "dev": dev},
+    )
+    swap.start()
+    swap.wait()
+    out_ref[...] = mine[...] + theirs[...]
+    for copy in partials:
+        copy.wait_send()
+    for n, copy in enumerate(copies):
+        if n == 0:
+            @pl.when(jnp.logical_not(keeps))
+            def _():
+                copies[0].wait_send()
+        else:
+            copy.wait_send()
+
+
+def dense(secs, devs, pooled, weights, bias, w_out):
+    n_bags, emb = pooled.shape
+    depth, hid = weights.shape
+    planes = devs // PLANE
+    group = n_bags // planes
+    block = group // PLANE
+    tiles = 4
+    vm = pl.BlockSpec(memory_space=pltpu.VMEM)
+    return pl.pallas_call(
+        functools.partial(dense_kernel, secs, devs),
+        out_shape=jax.ShapeDtypeStruct((1, block), jnp.float32),
+        in_specs=[vm] * 4,
+        out_specs=vm,
+        scratch_shapes=[
+            pltpu.VMEM((group, depth), jnp.bfloat16),
+            pltpu.VMEM((group, hid), jnp.float32),
+            pltpu.VMEM((group, hid), jnp.bfloat16),
+            pltpu.VMEM((PLANE - 1, block, hid), jnp.bfloat16),
+            pltpu.VMEM((1, block), jnp.float32),
+            pltpu.VMEM((1, block), jnp.float32),
+            pltpu.SemaphoreType.DMA((planes, secs)),
+            pltpu.SemaphoreType.DMA((depth // emb,)),
+            pltpu.SemaphoreType.DMA((PLANE - 1, tiles)),
+            pltpu.SemaphoreType.DMA((PLANE - 1, tiles)),
+            pltpu.SemaphoreType.DMA,
+            pltpu.SemaphoreType.DMA,
+        ],
+        compiler_params=pltpu.CompilerParams(collective_id=0, has_side_effects=True, vmem_limit_bytes=VMEM_LIMIT),
+        name="dense",
+    )(pooled, weights, bias, w_out)
 
 
 def body(indices, pool_len, tables, w_first, b_first, w_out):
@@ -14,16 +216,22 @@
     position = lax.axis_index("section") * dev_count + lax.axis_index("dev")
     table_id = position // row_split
     first_row = position % row_split * rows_dev
-    outgoing = jnp.repeat(indices, row_split, axis=1)
-    arrived = lax.all_to_all(outgoing, ("section", "dev"), split_axis=1, concat_axis=0, tiled=True)
+    outgoing = jnp.transpose(indices, (1, 0, 2)).reshape(n_tables, dev_rows * pool_size)
+    outgoing = jnp.repeat(outgoing, row_split, axis=0)
+    arrived = lax.all_to_all(outgoing, ("section", "dev"), split_axis=0, concat_axis=0, tiled=True)
     all_rows = devices * dev_rows
-    wanted = arrived.reshape(all_rows, pool_size) - first_row
+    wanted = arrived.reshape(all_rows * pool_size // 128, 128) - first_row
     live_slots = jnp.sum(jnp.where(jnp.arange(n_tables) == table_id, pool_len, 0))
-    usable = (wanted >= 0) & (wanted < rows_dev) & (jnp.arange(pool_size)[None, :] < live_slots)
-    safe_rows = jnp.where(usable, wanted, 0)
-    looked = jnp.take(tables, safe_rows, axis=0)
-    picked = jnp.where(usable[:, :, None], looked, jnp.zeros((), jnp.bfloat16))
-    partial_value = jnp.sum(picked.astype(jnp.float32), axis=1).astype(jnp.bfloat16)
+    slot = jnp.arange(128) % pool_size
+    usable = (wanted >= 0) & (wanted < rows_dev) & (slot < live_slots)[None, :]
+    safe_rows = jnp.where(usable, wanted, rows_dev)
+    partial_value = pool_bags(tables, safe_rows, pool_size)
+    planes = dev_count // PLANE
+    if row_split == 1 and sec_count == 2 and w_first.shape[0] % emb_width == 0 and dev_count % PLANE == 0:
+        columns = [[p * PLANE + i for p in range(planes)] for i in range(PLANE)]
+        near_weights = lax.all_gather(w_first, "dev", axis=0, tiled=True, axis_index_groups=columns)
+        logits = dense(sec_count, dev_count, partial_value, near_weights, b_first[None, :], w_out[None, :])
+        return logits.reshape(logits.shape[1])
     ordered = jnp.transpose(
         partial_value.reshape(dev_count, sec_count, dev_rows, emb_width), (1, 0, 2, 3)
     )

time: 337 us -> 166 us (0.49)
  waiting for transfers between devices: 204 us -> 46.7 us
  Pallas kernels: 0 us -> 91.6 us
  local copies, waits for them, and re-layouts: 64.5 us -> 5.48 us
  blocking collectives: 22.4 us -> 0 us
  other arithmetic: 15.6 us -> 2.58 us
  matrix products: 8.58 us -> 0 us
    all_gather x2 -> x1, waiting for transfers between devices: 201 us -> 46 us  [body(): lax.all_gather(w_first, 'dev', axis=0, tiled=True, axis_index_groups=colu...]
    pallas_call x0 -> x2, Pallas kernels: none -> 91.6 us  [the longest x1 69 us: dense(): pl.pallas_call(functools.partial(dense_kernel, secs, devs), out_shape=jax...]
    gather x1 -> x0, local copies, waits for them, and re-layouts: 59.4 us -> none  [body(): looked = jnp.take(tables, safe_rows, axis=0)]
    all_to_all x1 -> x0, blocking collectives: 18.4 us -> none  [body(): lax.all_to_all(ordered.reshape(devices, dev_rows, emb_width), ('section',...]
    reduce_sum x1 -> x0, other arithmetic: 12.6 us -> none  [body(): jnp.sum(picked.astype(jnp.float32), axis=1).astype(jnp.bfloat16)]
    dot_general x1 -> x0, matrix products: 8.58 us -> none  [body(): jnp.dot(samples, whole_weights, preferred_element_type=jnp.float32)]
    psum x1 -> x0, blocking collectives: 4.03 us -> none  [body(): return lax.psum(logit_part, 'section')]
  transfers between devices with their start and end apart: 3 -> 2, of which waited for: 3 -> 1; matrix products, arithmetic and copies ran while one was open for 1% -> 4% of each run, Pallas kernels for 0% -> 14%
where the time goes in v1:
time: 166 us
  Pallas kernels  91.6 us (55%)
  waiting for transfers between devices  46.7 us (28%)
  between operations  13.4 us (8%)
  starting transfers between devices  6.19 us (4%)
  local copies, waits for them, and re-layouts  5.48 us (3%)
  other arithmetic  2.58 us (2%)
    pallas_call x1, Pallas kernels, dense(): pl.pallas_call(functools.partial(dense_kernel, secs, devs), out_shape=jax...  69 us
    all_gather x1, waiting for transfers between devices, body(): lax.all_gather(w_first, 'dev', axis=0, tiled=True, axis_index_groups=colu...  46 us
    pallas_call x1, Pallas kernels, pool_bags(): pl.pallas_call(functools.partial(bag_kernel, chunks, bags_per_step, pool_...  22.6 us
    all_to_all x1, starting transfers between devices, body(): lax.all_to_all(outgoing, ('section', 'dev'), split_axis=0, concat_axis=0,...  6.19 us
  transfers between devices with their start and end apart: 2, of which 1 were waited for; matrix products, arithmetic and copies ran while one was open for 4% of the time, Pallas kernels for 14%

profile of v1, /device:TPU:19, one launch (start us, length us, event | category | flops | bytes accessed | tf_op | source)
XLA Modules:
  0.0 166.0 jit_solution(7178915735654557078)
XLA Ops:
  6.5 0.0 all-gather.2.cloned.1.call-start
  6.5 0.7 all-gather.2.cloned.1.call-update
  7.3 1.1 copy.9
  8.3 0.7 copy.10
  9.0 6.2 %all-to-all-start = ((s32[32,1,512]{2,1,0:T(1,128)}), s32[32,1,512]{2,1,0:T(1,128)S(1)}, u32[]{:S(2)}, u32[]{:S(2)}) async-start(s32[32,1,512]{2,1,0:T(1,128)} %copy.10), calls=%async_computation | async-start | bytes 131072 | tf_op jit(solution)/shard_map/all_to_all | solution.py:221
  15.2 1.3 fusion.1
  16.5 1.3 broadcast_in_dim.14.b_ref
  17.8 1.3 broadcast_in_dim.15.wo_ref
  19.1 0.7 fusion
  19.8 0.0 all-to-all-done
  19.8 0.6 and_select_fusion.ids_ref
  20.4 22.6 %pool_bags.1.pooled_ref = bf16[2048,128]{1,0:T(8,128)(2,1)} custom-call(bf16[32768,128]{1,0:T(8,128)(2,1)} %table_ref.1, s32[128,128]{1,0:T(8,128)} %and_select_fusion.ids_ref), custom_call_target="tpu_custom_call" | custom-call | flops 1258291200 | bytes 8388608 | tf_op jit(solution)/shard_map/pool_bags/pallas_call | solution.py:54
  43.1 46.0 %all-gather.2.cloned.1.call-done.w_ref = bf16[1024,2048]{1,0:T(8,128)(2,1)} async-done(((bf16[256,2048]{1,0:T(8,128)(2,1)}), bf16[1024,2048]{1,0:T(8,128)(2,1)}) %all-gather.2.cloned.1.call-update) | async-done | bytes 4194320 | tf_op jit(solution)/shard_map/all_gather | solution.py:232
  89.0 69.0 %dense.1 = f32[1,128]{1,0:T(1,128)} custom-call(bf16[2048,128]{1,0:T(8,128)(2,1)} %pool_bags.1.pooled_ref, bf16[1024,2048]{1,0:T(8,128)(2,1)} %all-gather.2.cloned.1.call-done.w_ref, bf16[1,2048]{1,0:T(2,128)(2,1)} %broadcast_in_dim.14.b_ref, bf16[1,2048]{1,0:T(2,128)(2,1)} %broadcast_in_dim.15.wo_ref), custom_call_target="tpu_custom_call" | custom-call | tf_op jit(solution)/shard_map/dense/pallas_call | solution.py:185
  158.0 1.1 copy.12
Async XLA Ops:
  6.5 82.5 %all-gather.2.cloned.1.call-start = ((), (), s32[]{:S(2)}) async-start(), calls=%async_computation.1 | async-start | bytes 5242880 | tf_op jit(solution)/shard_map/all_gather | solution.py:232
  9.0 10.8 %all-to-all-start = ((s32[32,1,512]{2,1,0:T(1,128)}), s32[32,1,512]{2,1,0:T(1,128)S(1)}, u32[]{:S(2)}, u32[]{:S(2)}) async-start(s32[32,1,512]{2,1,0:T(1,128)} %copy.10), calls=%async_computation | async-start | bytes 131072 | tf_op jit(solution)/shard_map/all_to_all | solution.py:221
Sparse Core Ops, SparseCore 0:
  8.9 80.1 all-gather.1

commit v2 on v1

--- a/solution.py
+++ b/solution.py
@@ -68,49 +68,124 @@
     )(table, ids)
 
 
-def dense_kernel(
-    secs, devs, pooled_ref, w_ref, b_ref, wo_ref, out_ref,
-    feats, pre, outgoing, incoming, mine, theirs,
-    fsend, frecv, psend, precv, lsend, lrecv,
+def step_kernel(
+    secs, devs, pool_size,
+    ids_ref, len_ref, table_ref, w_ref, b_ref, wo_ref, out_ref,
+    ids_in, ids_safe, ids_smem, staged, wide, sums, pooled, feats, weights, pre, outgoing, incoming, mine, theirs,
+    isend, irecv, icopy, tsem, fsend, frecv, wsend, wrecv, wlocal, psend, precv, lsend, lrecv,
 ):
-    emb = pooled_ref.shape[1]
-    depth, hid = w_ref.shape
-    per_dev = depth // (devs // PLANE)
+    rows, emb = table_ref.shape
+    count = secs * devs
+    per_dev, hid = w_ref.shape
+    depth = PLANE * per_dev
     tables_dev = per_dev // emb
     planes = devs // PLANE
-    group = pooled_ref.shape[0] // planes
-    block = group // PLANE
+    block = pooled.shape[2]
     tiles = psend.shape[1]
     tile = hid // tiles
     sec, dev = lax.axis_index("section"), lax.axis_index("dev")
     me = sec * devs + dev
-    plane, inner = dev // PLANE, dev % PLANE
+    plane, inner = dev // PLANE, lax.rem(dev, PLANE)
+
+    def device(position):
+        return {"section": position // devs, "dev": lax.rem(position, devs)}
+
+    chunks = 8
+    chunk = rows // chunks
+
+    def fetch(c):
+        return pltpu.make_async_copy(table_ref.at[pl.ds(c * chunk, chunk)], staged.at[c % 2], tsem.at[c % 2])
+
+    fetch(0).start()
+    own_weights = pltpu.make_async_copy(w_ref, weights.at[inner], wlocal)
+    own_weights.start()
+    own_ids = pltpu.make_async_copy(ids_ref.at[me], ids_in.at[me], irecv)
+    own_ids.start()
 
     barrier = pltpu.get_barrier_semaphore()
-    for k in range(1, secs * devs):
-        other = lax.rem(me + k, secs * devs)
-        pl.semaphore_signal(barrier, inc=1, device_id={"section": other // devs, "dev": lax.rem(other, devs)})
-    pl.semaphore_wait(barrier, secs * devs - 1)
-
+    for k in range(1, count):
+        pl.semaphore_signal(barrier, inc=1, device_id=device(lax.rem(me + k, count)))
+    pl.semaphore_wait(barrier, count - 1)
+
+    for k in range(1, count):
+        other = lax.rem(me + k, count)
+        pltpu.make_async_remote_copy(
+            src_ref=ids_ref.at[other], dst_ref=ids_in.at[me], send_sem=isend, recv_sem=irecv,
+            device_id=device(other),
+        ).start()
+
+    shipped = []
+
+    def ship(n):
+        cols = pl.ds(n * tile, tile)
+        for k in range(1, PLANE):
+            copy = pltpu.make_async_remote_copy(
+                src_ref=w_ref.at[:, cols], dst_ref=weights.at[inner, :, cols],
+                send_sem=wsend.at[k - 1, n], recv_sem=wrecv.at[k - 1, n],
+                device_id={"section": sec, "dev": plane * PLANE + lax.rem(inner + k, PLANE)},
+            )
+            copy.start()
+            shipped.append(copy)
+
+    ship(0)
+    ship(1)
+
+    wide[pl.ds(rows, 8), :] = jnp.zeros((8, emb), jnp.float32)
+    step = 256
+    for c in range(chunks):
+        if c + 1 < chunks:
+            fetch(c + 1).start()
+        fetch(c).wait()
+
+        def widen(k, carry):
+            at = pl.multiple_of(k * step, step)
+            wide[pl.ds(c * chunk + at, step), :] = staged[c % 2, pl.ds(at, step), :].astype(jnp.float32)
+            return carry
+
+        lax.fori_loop(0, chunk // step, widen, 0)
+
+    pltpu.make_async_copy(ids_in, ids_in, irecv).wait()
+    lane_slot = lax.rem(lax.broadcasted_iota(jnp.int32, ids_in.shape, 2), pool_size)
+    ids_safe[...] = jnp.where(lane_slot < len_ref[me], ids_in[...], rows)
+    to_smem = pltpu.make_async_copy(ids_safe, ids_smem, icopy)
+    to_smem.start()
+    to_smem.wait()
+
+    per_row = 128 // pool_size
+    id_rows = ids_in.shape[1]
+    block_rows = block // per_row
     owner = me // tables_dev
-    slot = owner // PLANE * tables_dev + lax.rem(me, tables_dev)
+    to_plane = owner // PLANE
+    slot = lax.rem(owner, PLANE) * tables_dev + lax.rem(me, tables_dev)
     column = pl.ds(pl.multiple_of(slot * emb, emb), emb)
-    to_inner = lax.rem(owner, PLANE)
-    keeps = to_inner == inner
+    keeps = to_plane == plane
     copies = []
-    for k in range(planes):
+    for k in list(range(1, PLANE)) + [0]:
+        to_inner = lax.rem(inner + k, PLANE)
+
+        def bags(n, carry):
+            at_plane, r = n // block_rows, lax.rem(n, block_rows)
+            line = (at_plane * PLANE + to_inner) * block_rows + r
+            source, part = line // id_rows, lax.rem(line, id_rows)
+            for q in range(per_row):
+                total = None
+                for p in range(pool_size):
+                    row = wide[pl.ds(ids_smem[source, part, q * pool_size + p], 1), :]
+                    total = row if total is None else total + row
+                sums[at_plane, to_inner, pl.ds(r * per_row + q, 1), :] = total
+            return carry
+
+        lax.fori_loop(0, planes * block_rows, bags, 0)
+        pooled[:, to_inner] = sums[:, to_inner].astype(jnp.bfloat16)
         for c in range(secs):
-            to_plane = lax.rem(plane + k, planes)
-            to_sec = lax.rem(sec + c, secs)
-            src = pooled_ref.at[pl.ds(pl.multiple_of(to_plane * group, group), group), :]
-            dst = feats.at[:, column]
+            source_part, dst = pooled.at[:, to_inner], feats.at[:, :, column]
             copy = pltpu.make_async_remote_copy(
-                src_ref=src, dst_ref=dst,
+                src_ref=source_part, dst_ref=dst,
                 send_sem=fsend.at[k, c], recv_sem=frecv.at[slot],
-                device_id={"section": to_sec, "dev": to_plane * PLANE + to_inner},
+                device_id={"section": lax.rem(sec + c, secs), "dev": to_plane * PLANE + to_inner},
             )
             if k == 0 and c == 0:
-                local = pltpu.make_async_copy(src, dst, frecv.at[slot])
+                local = pltpu.make_async_copy(source_part, dst, frecv.at[slot])
 
                 @pl.when(keeps)
                 def _():
@@ -119,37 +194,47 @@
                 @pl.when(jnp.logical_not(keeps))
                 def _():
                     copy.start()
+
+                kept = copy
             else:
                 copy.start()
-            copies.append(copy)
+                copies.append(copy)
+        if k == 1:
+            ship(2)
+        if k == 3:
+            ship(3)
     for t in range(depth // emb):
-        part = feats.at[:, pl.ds(t * emb, emb)]
+        part = feats.at[:, :, pl.ds(t * emb, emb)]
         pltpu.make_async_copy(part, part, frecv.at[t]).wait()
 
+    own_weights.wait()
     partials = []
     for n in range(tiles):
         cols = pl.ds(n * tile, tile)
-        got = jnp.dot(feats[...], w_ref[:, cols], preferred_element_type=jnp.float32)
-        pre[:, cols] = got
-        outgoing[:, cols] = got.astype(jnp.bfloat16)
         for k in range(1, PLANE):
-            to = lax.rem(inner + k, PLANE)
+            shipped[n * (PLANE - 1) + k - 1].wait_recv()
+        got = jnp.dot(
+            feats[...].reshape(planes * block, depth), weights[:, :, cols].reshape(depth, tile),
+            preferred_element_type=jnp.float32,
+        ).reshape(planes, block, tile)
+        pre[:, :, cols] = got
+        outgoing[:, :, cols] = got.astype(jnp.bfloat16)
+        for k in range(1, planes):
+            to = lax.rem(plane + k, planes)
             copy = pltpu.make_async_remote_copy(
-                src_ref=outgoing.at[pl.ds(pl.multiple_of(to * block, block), block), cols],
-                dst_ref=incoming.at[k - 1, :, cols],
+                src_ref=outgoing.at[to, :, cols], dst_ref=incoming.at[k - 1, :, cols],
                 send_sem=psend.at[k - 1, n], recv_sem=precv.at[k - 1, n],
-                device_id={"section": sec, "dev": plane * PLANE + to},
+                device_id={"section": sec, "dev": to * PLANE + inner},
             )
             copy.start()
             partials.append(copy)
 
     acc = jnp.zeros((block, 128), jnp.float32)
-    own = pl.ds(pl.multiple_of(inner * block, block), block)
     for n in range(tiles):
         cols = pl.ds(n * tile, tile)
-        total = pre[own, cols]
-        for k in range(1, PLANE):
-            partials[n * (PLANE - 1) + k - 1].wait_recv()
+        total = pre[plane, :, cols]
+        for k in range(1, planes):
+            partials[n * (planes - 1) + k - 1].wait_recv()
             total = total + incoming[k - 1, :, cols].astype(jnp.float32)
         hidden = jnp.maximum(total + b_ref[:, cols].astype(jnp.float32), 0.0)
         weighed = hidden * wo_ref[:, cols].astype(jnp.float32)
@@ -163,47 +248,57 @@
     swap.start()
     swap.wait()
     out_ref[...] = mine[...] + theirs[...]
-    for copy in partials:
+    for copy in partials + shipped + copies:
         copy.wait_send()
-    for n, copy in enumerate(copies):
-        if n == 0:
-            @pl.when(jnp.logical_not(keeps))
-            def _():
-                copies[0].wait_send()
-        else:
-            copy.wait_send()
-
-
-def dense(secs, devs, pooled, weights, bias, w_out):
-    n_bags, emb = pooled.shape
-    depth, hid = weights.shape
+
+    @pl.when(jnp.logical_not(keeps))
+    def _():
+        kept.wait_send()
+
+    sent = ids_in.at[pl.ds(0, count - 1)]
+    pltpu.make_async_copy(sent, sent, isend).wait()
+
+
+def whole_step(secs, devs, pool_size, ids, pool_len, table, w_first, bias, w_out):
+    rows, emb = table.shape
+    per_dev, hid = w_first.shape
+    count = secs * devs
     planes = devs // PLANE
-    group = n_bags // planes
-    block = group // PLANE
+    depth = PLANE * per_dev
+    block = ids.shape[1] * 128 // pool_size * secs
     tiles = 4
     vm = pl.BlockSpec(memory_space=pltpu.VMEM)
+    anywhere = pl.BlockSpec(memory_space=pl.ANY)
+    dma = pltpu.SemaphoreType.DMA
     return pl.pallas_call(
-        functools.partial(dense_kernel, secs, devs),
+        functools.partial(step_kernel, secs, devs, pool_size),
         out_shape=jax.ShapeDtypeStruct((1, block), jnp.float32),
-        in_specs=[vm] * 4,
+        in_specs=[vm, pl.BlockSpec(memory_space=pltpu.SMEM), anywhere, anywhere, vm, vm],
         out_specs=vm,
         scratch_shapes=[
-            pltpu.VMEM((group, depth), jnp.bfloat16),
-            pltpu.VMEM((group, hid), jnp.float32),
-            pltpu.VMEM((group, hid), jnp.bfloat16),
-            pltpu.VMEM((PLANE - 1, block, hid), jnp.bfloat16),
+            pltpu.VMEM(ids.shape, jnp.int32),
+            pltpu.VMEM(ids.shape, jnp.int32),
+            pltpu.SMEM(ids.shape, jnp.int32),
+            pltpu.VMEM((2, rows // 8, emb), jnp.bfloat16),
+            pltpu.VMEM((rows + 8, emb), jnp.float32),
+            pltpu.VMEM((planes, PLANE, block, emb), jnp.float32),
+            pltpu.VMEM((planes, PLANE, block, emb), jnp.bfloat16),
+            pltpu.VMEM((planes, block, depth), jnp.bfloat16),
+            pltpu.VMEM((PLANE, per_dev, hid), jnp.bfloat16),
+            pltpu.VMEM((planes, block, hid), jnp.float32),
+            pltpu.VMEM((planes, block, hid), jnp.bfloat16),
+            pltpu.VMEM((planes - 1, block, hid), jnp.bfloat16),
             pltpu.VMEM((1, block), jnp.float32),
             pltpu.VMEM((1, block), jnp.float32),
-            pltpu.SemaphoreType.DMA((planes, secs)),
-            pltpu.SemaphoreType.DMA((depth // emb,)),
-            pltpu.SemaphoreType.DMA((PLANE - 1, tiles)),
-            pltpu.SemaphoreType.DMA((PLANE - 1, tiles)),
-            pltpu.SemaphoreType.DMA,
-            pltpu.SemaphoreType.DMA,
+            dma, dma, dma, dma((2,)),
+            dma((PLANE, secs)), dma((depth // emb,)),
+            dma((PLANE - 1, tiles)), dma((PLANE - 1, tiles)), dma,
+            dma((planes - 1, tiles)), dma((planes - 1, tiles)),
+            dma, dma,
         ],
         compiler_params=pltpu.CompilerParams(collective_id=0, has_side_effects=True, vmem_limit_bytes=VMEM_LIMIT),
-        name="dense",
-    )(pooled, weights, bias, w_out)
+        name="whole_step",
+    )(ids, pool_len, table, w_first, bias, w_out)
 
 
 def body(indices, pool_len, tables, w_first, b_first, w_out):
@@ -217,6 +312,13 @@
     table_id = position // row_split
     first_row = position % row_split * rows_dev
     outgoing = jnp.transpose(indices, (1, 0, 2)).reshape(n_tables, dev_rows * pool_size)
+    square = row_split == 1 and sec_count == 2 and dev_count % PLANE == 0
+    if square and w_first.shape[0] % emb_width == 0 and dev_rows * pool_size % 128 == 0:
+        ids = outgoing.reshape(n_tables, dev_rows * pool_size // 128, 128)
+        logits = whole_step(
+            sec_count, dev_count, pool_size, ids, pool_len, tables, w_first, b_first[None, :], w_out[None, :]
+        )
+        return logits.reshape(logits.shape[1])
     outgoing = jnp.repeat(outgoing, row_split, axis=0)
     arrived = lax.all_to_all(outgoing, ("section", "dev"), split_axis=0, concat_axis=0, tiled=True)
     all_rows = devices * dev_rows
@@ -226,12 +328,6 @@
     usable = (wanted >= 0) & (wanted < rows_dev) & (slot < live_slots)[None, :]
     safe_rows = jnp.where(usable, wanted, rows_dev)
     partial_value = pool_bags(tables, safe_rows, pool_size)
-    planes = dev_count // PLANE
-    if row_split == 1 and sec_count == 2 and w_first.shape[0] % emb_width == 0 and dev_count % PLANE == 0:
-        columns = [[p * PLANE + i for p in range(planes)] for i in range(PLANE)]
-        near_weights = lax.all_gather(w_first, "dev", axis=0, tiled=True, axis_index_groups=columns)
-        logits = dense(sec_count, dev_count, partial_value, near_weights, b_first[None, :], w_out[None, :])
-        return logits.reshape(logits.shape[1])
     ordered = jnp.transpose(
         partial_value.reshape(dev_count, sec_count, dev_rows, emb_width), (1, 0, 2, 3)
     )

time: 166 us -> 102 us (0.61)
  the two profiles are of different devices: /device:TPU:19 before, /device:TPU:25 now
where the time goes in v2:
time: 102 us
  Pallas kernels  96.1 us (94%)
  local copies, waits for them, and re-layouts  5.46 us (5%)
    pallas_call x1, Pallas kernels, whole_step(): pl.pallas_call(functools.partial(step_kernel, secs, devs, pool_size), out...  96.1 us

profile of v2, /device:TPU:25, one launch (start us, length us, event | category | flops | bytes accessed | tf_op | source)
XLA Modules:
  0.0 101.6 jit_solution(2327291653107940382)
XLA Ops:
  0.0 1.1 %copy.8 = s32[32,64,8]{0,2,1:T(8,128)S(1)} copy(s32[32,64,8]{1,2,0:T(8,128)} %bitcast.4) | data formatting | bytes 131072 | tf_op jit(solution)/shard_map/transpose | solution.py:314
  1.1 0.7 copy.9.ids_ref
  1.8 1.3 %broadcast_in_dim.6.b_ref = bf16[1,2048]{1,0:T(2,128)(2,1)} reshape(bf16[2048]{0:T(1024)(128)(2,1)} %param.10) | data formatting | bytes 8192 | tf_op jit(solution)/shard_map/broadcast_in_dim | solution.py:319
  3.1 1.3 %broadcast_in_dim.7.wo_ref = bf16[1,2048]{1,0:T(2,128)(2,1)} reshape(bf16[2048]{0:T(1024)(128)(2,1)} %param.11) | data formatting | bytes 8192 | tf_op jit(solution)/shard_map/broadcast_in_dim | solution.py:319
  4.4 96.1 %whole_step.1 = f32[1,128]{1,0:T(1,128)} custom-call(s32[32,4,128]{2,1,0:T(4,128)} %copy.9.ids_ref, s32[32]{0:T(128)} %len_ref.1, bf16[32768,128]{1,0:T(8,128)(2,1)} %table_ref.1, bf16[256,2048]{1,0:T(8,128)(2,1)} %w_ref.1, bf16[1,2048]{1,0:T(2,128)(2,1)} %broadcast_in_dim.6.b_ref, bf16[1,2048]{1,0:T(2,128)(2,1)} %broadcast_in_dim.7.wo_ref), custom_call_target="tpu_custom_call" | custom-call | tf_op jit(solution)/shard_map/whole_step/pallas_call | solution.py:273
  100.5 1.1 %copy.11 = f32[128]{0:T(128)} copy(f32[128]{0:T(128)} %bitcast.5) | data formatting | bytes 1024

commit v3 on v2

--- a/solution.py
+++ b/solution.py
@@ -9,6 +9,7 @@
 
 VMEM_LIMIT = 60 * 1024 * 1024
 PLANE = 4
+PLANES = 4
 
 
 def bag_kernel(table_chunks, bags_per_step, pool_size, table_ref, ids_ref, out_ref, staged, wide, sums, sems):
@@ -71,7 +72,7 @@
 def step_kernel(
     secs, devs, pool_size,
     ids_ref, len_ref, table_ref, w_ref, b_ref, wo_ref, out_ref,
-    ids_in, ids_safe, ids_smem, staged, wide, sums, pooled, feats, weights, pre, outgoing, incoming, mine, theirs,
+    ids_in, ids_safe, ids_smem, staged, wide, sums, pooled, feats, weights, pre, outgoing, relay, incoming, mine, theirs,
     isend, irecv, icopy, tsem, fsend, frecv, wsend, wrecv, wlocal, psend, precv, lsend, lrecv,
 ):
     rows, emb = table_ref.shape
@@ -127,8 +128,8 @@
             copy.start()
             shipped.append(copy)
 
-    ship(0)
-    ship(1)
+    for n in range(tiles // 2):
+        ship(n)
 
     wide[pl.ds(rows, 8), :] = jnp.zeros((8, emb), jnp.float32)
     step = 256
@@ -199,16 +200,37 @@
             else:
                 copy.start()
                 copies.append(copy)
-        if k == 1:
-            ship(2)
-        if k == 3:
-            ship(3)
+        if k == PLANE - 1:
+            for n in range(tiles // 2, 3 * tiles // 4):
+                ship(n)
+        if k == 0:
+            for n in range(3 * tiles // 4, tiles):
+                ship(n)
     for t in range(depth // emb):
         part = feats.at[:, :, pl.ds(t * emb, emb)]
         pltpu.make_async_copy(part, part, frecv.at[t]).wait()
 
     own_weights.wait()
-    partials = []
+    near = plane + 1 - 2 * lax.rem(plane, 2)
+    far = lax.rem(plane + 2, PLANES)
+    partials = {}
+
+    def send(src, lane, n, to):
+        cols = pl.ds(n * tile, tile)
+        copy = pltpu.make_async_remote_copy(
+            src_ref=src, dst_ref=incoming.at[lane, :, cols],
+            send_sem=psend.at[lane, n], recv_sem=precv.at[lane, n],
+            device_id={"section": sec, "dev": to * PLANE + inner},
+        )
+        copy.start()
+        partials[lane, n] = copy
+
+    def pass_on(n):
+        cols = pl.ds(n * tile, tile)
+        partials[1, n].wait_recv()
+        relay[:, cols] = (pre[far, :, cols] + incoming[1, :, cols].astype(jnp.float32)).astype(jnp.bfloat16)
+        send(relay.at[:, cols], 2, n, far)
+
     for n in range(tiles):
         cols = pl.ds(n * tile, tile)
         for k in range(1, PLANE):
@@ -219,25 +241,22 @@
         ).reshape(planes, block, tile)
         pre[:, :, cols] = got
         outgoing[:, :, cols] = got.astype(jnp.bfloat16)
-        for k in range(1, planes):
-            to = lax.rem(plane + k, planes)
-            copy = pltpu.make_async_remote_copy(
-                src_ref=outgoing.at[to, :, cols], dst_ref=incoming.at[k - 1, :, cols],
-                send_sem=psend.at[k - 1, n], recv_sem=precv.at[k - 1, n],
-                device_id={"section": sec, "dev": to * PLANE + inner},
-            )
-            copy.start()
-            partials.append(copy)
+        send(outgoing.at[lax.rem(near + 2, PLANES), :, cols], 1, n, near)
+        send(outgoing.at[near, :, cols], 0, n, near)
+        if n >= 2:
+            pass_on(n - 2)
+    pass_on(tiles - 2)
+    pass_on(tiles - 1)
 
     acc = jnp.zeros((block, 128), jnp.float32)
     for n in range(tiles):
         cols = pl.ds(n * tile, tile)
         total = pre[plane, :, cols]
-        for k in range(1, planes):
-            partials[n * (planes - 1) + k - 1].wait_recv()
-            total = total + incoming[k - 1, :, cols].astype(jnp.float32)
-        hidden = jnp.maximum(total + b_ref[:, cols].astype(jnp.float32), 0.0)
-        weighed = hidden * wo_ref[:, cols].astype(jnp.float32)
+        for lane in (0, 2):
+            partials[lane, n].wait_recv()
+            total = total + incoming[lane, :, cols].astype(jnp.float32)
+        hidden = jnp.maximum(total + b_ref[cols].astype(jnp.float32)[None, :], 0.0)
+        weighed = hidden * wo_ref[cols].astype(jnp.float32)[None, :]
         for q in range(tile // 128):
             acc = acc + weighed[:, q * 128:(q + 1) * 128]
     mine[...] = jnp.sum(acc.T, axis=0, keepdims=True)
@@ -248,7 +267,7 @@
     swap.start()
     swap.wait()
     out_ref[...] = mine[...] + theirs[...]
-    for copy in partials + shipped + copies:
+    for copy in list(partials.values()) + shipped + copies:
         copy.wait_send()
 
     @pl.when(jnp.logical_not(keeps))
@@ -266,7 +285,7 @@
     planes = devs // PLANE
     depth = PLANE * per_dev
     block = ids.shape[1] * 128 // pool_size * secs
-    tiles = 4
+    tiles = 8
     vm = pl.BlockSpec(memory_space=pltpu.VMEM)
     anywhere = pl.BlockSpec(memory_space=pl.ANY)
     dma = pltpu.SemaphoreType.DMA
@@ -287,13 +306,14 @@
             pltpu.VMEM((PLANE, per_dev, hid), jnp.bfloat16),
             pltpu.VMEM((planes, block, hid), jnp.float32),
             pltpu.VMEM((planes, block, hid), jnp.bfloat16),
-            pltpu.VMEM((planes - 1, block, hid), jnp.bfloat16),
+            pltpu.VMEM((block, hid), jnp.bfloat16),
+            pltpu.VMEM((3, block, hid), jnp.bfloat16),
             pltpu.VMEM((1, block), jnp.float32),
             pltpu.VMEM((1, block), jnp.float32),
             dma, dma, dma, dma((2,)),
             dma((PLANE, secs)), dma((depth // emb,)),
             dma((PLANE - 1, tiles)), dma((PLANE - 1, tiles)), dma,
-            dma((planes - 1, tiles)), dma((planes - 1, tiles)),
+            dma((3, tiles)), dma((3, tiles)),
             dma, dma,
         ],
         compiler_params=pltpu.CompilerParams(collective_id=0, has_side_effects=True, vmem_limit_bytes=VMEM_LIMIT),
@@ -312,11 +332,11 @@
     table_id = position // row_split
     first_row = position % row_split * rows_dev
     outgoing = jnp.transpose(indices, (1, 0, 2)).reshape(n_tables, dev_rows * pool_size)
-    square = row_split == 1 and sec_count == 2 and dev_count % PLANE == 0
+    square = row_split == 1 and sec_count == 2 and dev_count == PLANE * PLANES
     if square and w_first.shape[0] % emb_width == 0 and dev_rows * pool_size % 128 == 0:
         ids = outgoing.reshape(n_tables, dev_rows * pool_size // 128, 128)
         logits = whole_step(
-            sec_count, dev_count, pool_size, ids, pool_len, tables, w_first, b_first[None, :], w_out[None, :]
+            sec_count, dev_count, pool_size, ids, pool_len, tables, w_first, b_first, w_out
         )
         return logits.reshape(logits.shape[1])
     outgoing = jnp.repeat(outgoing, row_split, axis=0)

time: 102 us -> 89.6 us (0.88)
  the two profiles are of different devices: /device:TPU:25 before, /device:TPU:19 now
where the time goes in v3:
time: 89.6 us; the launch traced here: 88.7 us
  Pallas kernels  85.8 us (96%)
  local copies, waits for them, and re-layouts  2.93 us (3%)
    pallas_call x1, Pallas kernels, whole_step(): pl.pallas_call(functools.partial(step_kernel, secs, devs, pool_size), out...  85.8 us

profile of v3, /device:TPU:19, one launch (start us, length us, event | category | flops | bytes accessed | tf_op | source)
XLA Modules:
  0.0 88.7 jit_solution(15373076269367530586)
XLA Ops:
  0.0 1.1 %copy.8 = s32[32,64,8]{0,2,1:T(8,128)S(1)} copy(s32[32,64,8]{1,2,0:T(8,128)} %bitcast.4) | data formatting | bytes 131072 | tf_op jit(solution)/shard_map/transpose | solution.py:334
  1.1 0.7 copy.9.ids_ref
  1.8 85.8 %whole_step.1 = f32[1,128]{1,0:T(1,128)} custom-call(s32[32,4,128]{2,1,0:T(4,128)} %copy.9.ids_ref, s32[32]{0:T(128)} %len_ref.1, bf16[32768,128]{1,0:T(8,128)(2,1)} %table_ref.1, bf16[256,2048]{1,0:T(8,128)(2,1)} %w_ref.1, bf16[2048]{0:T(1024)(128)(2,1)} %b_ref.1, bf16[2048]{0:T(1024)(128)(2,1)} %wo_ref.1), custom_call_target="tpu_custom_call" | custom-call | tf_op jit(solution)/shard_map/whole_step/pallas_call | solution.py:292
  87.6 1.1 %copy.11 = f32[128]{0:T(128)} copy(f32[128]{0:T(128)} %bitcast.5) | data formatting | bytes 1024
